TPU v7x, 32 devices: a whole 2x2x4 slice. The times are simulated.
32 devices in a mesh: lat: 4 (over x, core), lon: 8 (over z, y).
Axes of the slice: x: 2, y: 2, z: 4, core: 2. Of those that a mesh axis runs over, the one named last changes fastest.
Arguments:
- tokens: bfloat16 [4, 56, 32, 1536], P(None, 'lat', 'lon'), may hold values from -400 to 400, as said below
- in_bounds: int32 [5], replicated, may hold values from 0 to 47, as said below
- out_bounds: int32 [5], replicated, may hold values from 0 to 24, as said below
- down_gain: float32 [768], replicated, may hold values from 0.25 to 1.75
- down_bias: float32 [768], replicated, may hold values from -1 to 1
- down_weight: bfloat16 [768, 384], replicated, may hold values from -0.21875 to 0.21875
- up_weight: bfloat16 [384, 768], replicated, may hold values from -0.3125 to 0.3125
- up_gain: float32 [192], replicated, may hold values from 0.25 to 1.75
- up_bias: float32 [192], replicated, may hold values from -1 to 1
- out_weight: bfloat16 [192, 192], replicated, may hold values from -0.4375 to 0.4375
Outputs:
- merged: bfloat16 [4, 32, 16, 3072], P(None, 'lat', 'lon')
- upsampled: bfloat16 [4, 56, 32, 1536], P(None, 'lat', 'lon')
Inputs may be any that keep to these rules, and one draw needn't show every extreme that they name: `tokens`: band b's fine rows stand in its slots from the first one on; slots past the band's count hold values that no output reads. in_bounds[0] = 0, in_bounds[4] = 47; each band has 10 to 14 fine rows, and some band has 14. out_bounds[0] = 0, out_bounds[4] = 24; each band has 4 to 8 merged rows, and some band has 8. For 0 < b < 4, 2 * out_bounds[b] - in_bounds[b] is 1 to 3, and 3 for some b; so merged band b covers fine rows from band b's first on to at most 3 rows past its last (fine row 47 counting as zeros), and band b's fine rows need merged rows from at most 2 rows before merged band b's first up to its last, 2 being reached.
All inputs are finite; a program needn't handle non-finite values.
Results may differ from a plain program's by a relative error of at most 0.0069.
Values may be sent and summed in bfloat16 or wider, within the bound.
A program may use at most 64 MiB of HBM per device.

v0:
```python
import jax
import jax.numpy as jnp
from jax import lax
from jax.sharding import PartitionSpec as P

HALO = 3


def passed_along(value, axis, steps):
    count = lax.axis_size(axis)
    leading, last = (max(0, -steps), min(count, count - steps))
    return lax.ppermute(value, axis, [(source, source + steps) for source in range(leading, last)])


def passed_along_2(value, axis, by):
    size = lax.axis_size(axis)
    return lax.ppermute(value, axis, [(i, (i + by) % size) for i in range(size)])


def layer_norm(values, scale_vec, shift_vec):
    center = jnp.mean(values, axis=-1, keepdims=True)
    spread = jnp.mean(jnp.square(values - center), axis=-1, keepdims=True)
    return (values - center) * lax.rsqrt(spread + 1e-05) * scale_vec + shift_vec


def body(
    tokens,
    in_bounds,
    out_bounds,
    down_gain,
    down_bias,
    down_weight,
    up_weight,
    up_gain,
    up_bias,
    out_weight,
):
    members, slot_rows, columns, packed = tokens.shape
    channels = down_weight.shape[0] // 4
    levels = packed // channels
    merged_slots = slot_rows // 2 + 1
    half_cols = columns // 2
    band_index = lax.axis_index("lat")
    start_in = in_bounds[band_index]
    end_in = in_bounds[band_index + 1]
    start_out = out_bounds[band_index]
    end_out = out_bounds[band_index + 1]
    count_in = end_in - start_in
    count_out = end_out - start_out
    head_rows = tokens[:, :HALO]
    from_below = passed_along(head_rows, "lat", -1)
    stacked = jnp.concatenate([tokens, from_below], axis=1)
    wanted = 2 * start_out + jnp.arange(2 * merged_slots, dtype=jnp.int32)
    position = jnp.where(wanted < end_in, wanted - start_in, wanted - end_in + slot_rows)
    position = jnp.clip(position, 0, slot_rows + HALO - 1)
    extended = jnp.take(stacked, position, axis=1)
    left_edge = passed_along_2(extended[:, :, columns - 1], "lon", 1)
    shifted = jnp.concatenate([left_edge[:, :, None], extended[:, :, : columns - 1]], axis=2)
    pieces = shifted.reshape(members, merged_slots, 2, half_cols, 2, levels, channels)
    pieces = pieces.transpose(0, 1, 3, 5, 4, 2, 6).reshape(-1, 4 * channels)
    normed = layer_norm(pieces.astype(jnp.float32), down_gain, down_bias).astype(jnp.bfloat16)
    merged = jnp.dot(normed, down_weight, preferred_element_type=jnp.float32).astype(jnp.bfloat16)
    merged = merged.reshape(members, merged_slots, half_cols, levels * 2 * channels)
    merged_live = jnp.arange(merged_slots, dtype=jnp.int32) < count_out
    merged = jnp.where(merged_live[None, :, None, None], merged, jnp.zeros((), jnp.bfloat16))
    widened = jnp.dot(
        merged.reshape(-1, 2 * channels), up_weight, preferred_element_type=jnp.float32
    ).astype(jnp.bfloat16)
    widened = widened.reshape(members, merged_slots, half_cols, levels, 2, 2, channels)
    right_edge = passed_along_2(widened[:, :, 0, :, 0], "lon", -1)
    spread_out = widened.transpose(0, 1, 5, 2, 4, 3, 6).reshape(
        members, 2 * merged_slots, columns, packed
    )
    edge_rows = right_edge.transpose(0, 1, 3, 2, 4).reshape(members, 2 * merged_slots, packed)
    expanded = jnp.concatenate([spread_out[:, :, 1:], edge_rows[:, :, None]], axis=2)
    tail_fine = lax.dynamic_slice_in_dim(expanded, 2 * count_out - HALO, HALO, 1)
    fine_up = passed_along(tail_fine, "lat", 1)
    stacked_fine = jnp.concatenate([fine_up, expanded], axis=1)
    wanted_fine = start_in + jnp.arange(slot_rows, dtype=jnp.int32)
    spot = jnp.clip(wanted_fine - 2 * start_out + HALO, 0, 2 * merged_slots + HALO - 1)
    fine_rows = jnp.take(stacked_fine, spot, axis=1)
    fine_levels = fine_rows.reshape(members, slot_rows, columns, levels, channels)
    renormed = layer_norm(fine_levels.astype(jnp.float32), up_gain, up_bias).astype(jnp.bfloat16)
    finished = jnp.dot(
        renormed.reshape(-1, channels), out_weight, preferred_element_type=jnp.float32
    ).astype(jnp.bfloat16)
    finished = finished.reshape(members, slot_rows, columns, packed)
    fine_live = jnp.arange(slot_rows, dtype=jnp.int32) < count_in
    upsampled = jnp.where(fine_live[None, :, None, None], finished, jnp.zeros((), jnp.bfloat16))
    return (merged, upsampled)


def solution(mesh):
    return jax.shard_map(
        body,
        mesh=mesh,
        in_specs=(P(None, "lat", "lon", None), P(), P(), P(), P(), P(), P(), P(), P(), P()),
        out_specs=(P(None, "lat", "lon", None), P(None, "lat", "lon", None)),
        check_vma=False,
    )
```

profile of v0, /device:TPU:1, one launch (start us, length us, event | category | flops | bytes accessed | tf_op | source)
XLA Modules:
  0.0 73.7 jit_solution(7933006558912201801)
XLA Ops:
  0.6 1.0 %slice.15 = bf16[4,3,4,1536]{3,2,1,0:T(4,128)(2,1)S(1)} slice(bf16[4,14,4,1536]{3,2,1,0:T(4,128)(2,1)} %param.10), slice={[0:4], [0:3], [0:4], [0:1536]} | slice | bytes 294912 | tf_op jit(solution)/shard_map/slice | solution.py:50
  1.7 1.9 %collective-permute-start = (bf16[4,3,4,1536]{3,2,1,0:T(4,128)(2,1)S(1)}, bf16[4,3,4,1536]{3,2,1,0:T(4,128)(2,1)S(1)}, u32[]{:S(2)}, u32[]{:S(2)}) collective-permute-start(bf16[4,3,4,1536]{3,2,1,0:T(4,128)(2,1)S(1)} %slice.15), channel_id=1, source_target_pairs={{8,0},{16,8},{24,16},{9,1},{17,9},{25,17},{10,2},{18,10},{26,18},{... | collective-permute-start | bytes 442376 | tf_op jit(solution)/shard_map/ppermute | solution.py:12
  3.6 1.4 %fusion.23 = (s32[1]{0:T(128)}, s32[1]{0:T(128)}, s32[1]{0:T(128)}, s32[1]{0:T(128)}) fusion(s32[5]{0:T(128)} %param.12, s32[]{:T(128)S(6)} %select_n.80, s32[]{:T(128)S(6)} %select_n.81, s32[5]{0:T(128)} %param.11), kind=kLoop, calls=%fused_computation.62 | loop fusion | bytes 40 | tf_op jit(solution)/shard_map/dynamic_slice | solution.py:47
  5.7 1.3 %fusion.18 = s32[16]{0:T(128)S(1)} fusion(s32[]{:T(128)} %bitcast.3, s32[]{:T(128)} %bitcast.2, s32[]{:T(128)} %bitcast.1), kind=kLoop, calls=%fused_computation.55 | loop fusion | flops 160 | bytes 76 | tf_op jit(solution)/shard_map/jit(_take)/jit(_where)/select_n | solution.py:56
  6.9 1.3 %compare_and_fusion.1 = pred[16]{0:T(512)(128)(4,1)S(1)} fusion(s32[]{:T(128)} %bitcast.3, s32[]{:T(128)} %bitcast.2, s32[]{:T(128)} %bitcast.1), kind=kLoop, calls=%fused_computation.51 | loop fusion | flops 208 | bytes 28 | tf_op jit(solution)/shard_map/jit(_take)/and | solution.py:56
  10.8 0.3 broadcast_in_dim.69
  11.0 0.5 broadcast_in_dim.78
  11.6 1.6 %pad_maximum_fusion = bf16[4,17,4,1536]{3,2,1,0:T(4,128)(2,1)S(1)} fusion(bf16[4,3,4,1536]{3,2,1,0:T(4,128)(2,1)S(1)} %collective-permute-done, bf16[4,14,4,1536]{3,2,1,0:T(4,128)(2,1)} %param.10), kind=kLoop, calls=%fused_computation.22 | loop fusion | flops 417792 | bytes 1671168 | tf_op jit(solution)/shard_map/concatenate | solution.py:52
  13.2 1.2 %gather_fusion = bf16[16,4,4,1536]{3,2,1,0:T(4,128)(2,1)S(1)} fusion(bf16[4,17,4,1536]{3,2,1,0:T(4,128)(2,1)S(1)} %pad_maximum_fusion, s32[1024]{0:T(1024)S(1)} %pad_clamp_fusion.1), kind=kCustom, calls=%fused_computation | custom fusion | bytes 1572928 | tf_op jit(solution)/shard_map/jit(_take)/gather | solution.py:56
  14.5 0.4 select_bitcast_fusion
  14.9 0.4 slice.24
  15.5 2.8 %collective-permute-start.1 = (bf16[4,16,1536]{2,1,0:T(8,128)(2,1)S(1)}, bf16[4,16,1536]{2,1,0:T(8,128)(2,1)S(1)}, u32[]{:S(2)}, u32[]{:S(2)}) collective-permute-start(bf16[4,16,1536]{2,1,0:T(8,128)(2,1)S(1)} %bitcast.48), channel_id=1, source_target_pairs={{0,1},{1,2},{2,3},{3,4},{4,5},{5,6},{6,7},{7,0},{8,9},{9,10},{10,1... | collective-permute-start | bytes 589832 | tf_op jit(solution)/shard_map/ppermute | solution.py:17
  18.2 0.7 compare_and_fusion
  19.2 0.7 fusion.19
  19.9 6.2 %collective-permute-done.1 = bf16[4,16,1536]{2,1,0:T(8,128)(2,1)S(1)} collective-permute-done((bf16[4,16,1536]{2,1,0:T(8,128)(2,1)S(1)}, bf16[4,16,1536]{2,1,0:T(8,128)(2,1)S(1)}, u32[]{:S(2)}, u32[]{:S(2)}) %collective-permute-start.1) | collective-permute-done | bytes 196640 | tf_op jit(solution)/shard_map/ppermute | solution.py:17
  26.0 0.3 copy.53
  26.3 1.9 %maximum_convert_fusion = f32[4,16,4,1536]{3,2,0,1:T(4,128)} fusion(bf16[4,16,3,1536]{3,2,0,1:T(4,128)(2,1)S(1)} %bitcast.46, bf16[4,16,1,1536]{3,2,0,1:T(2,128)(2,1)S(1)} %copy.53), kind=kLoop, calls=%fused_computation.23 | loop fusion | flops 1572864 | bytes 2359296 | tf_op jit(solution)/shard_map/convert_element_type | solution.py:61
  28.3 2.2 %reshape.178 = f32[4,8,2,2,2,8,192]{6,5,4,3,0,2,1:T(8,128)S(1)} reshape(f32[4,16,4,1536]{3,2,0,1:T(4,128)} %maximum_convert_fusion) | data formatting | bytes 3145728 | tf_op jit(solution)/shard_map/convert_element_type | solution.py:61
  30.4 2.4 %fusion.22 = f32[4,8,2,8]{3,2,1,0:T(2,128)S(1)} fusion(f32[4,8,2,2,2,8,192]{6,5,4,3,0,2,1:T(8,128)S(1)} %reshape.178), kind=kLoop, calls=%fused_computation.61 | loop fusion | flops 392704 | bytes 1574912 | tf_op jit(solution)/shard_map/reduce_sum | solution.py:21
  32.9 3.3 %copy.76 = f32[4,8,2,2,2,8,192]{6,2,4,5,3,1,0:T(2,128)} copy(f32[4,8,2,2,2,8,192]{6,5,4,3,0,2,1:T(8,128)S(1)} %reshape.178) | data formatting | bytes 3145728 | tf_op jit(solution)/shard_map/convert_element_type | solution.py:61
  36.2 2.6 %multiply_reduce_fusion = f32[4,8,2,8]{3,2,1,0:T(2,128)S(1)} fusion(f32[4,8,2,8]{3,2,1,0:T(2,128)S(1)} %broadcast_multiply_fusion.1, f32[4,8,2,2,2,8,192]{6,5,4,3,0,2,1:T(8,128)S(1)} %reshape.178), kind=kLoop, calls=%fused_computation.6 | loop fusion | flops 1179136 | bytes 1576960 | tf_op jit(solution)/shard_map/reduce_sum | solution.py:22
  39.1 3.2 %reshape.176 = f32[512,768]{1,0:T(8,128)S(1)} reshape(f32[4,8,2,8,2,2,192]{6,5,4,3,2,1,0:T(2,128)} %bitcast.43) | data formatting | bytes 3145728 | tf_op jit(solution)/shard_map/convert_element_type | solution.py:61
  42.3 1.7 %convolution_convert_fusion.2 = bf16[512,384]{1,0:T(8,128)(2,1)S(1)} fusion(bf16[768,384]{1,0:T(8,128)(2,1)} %param.15, f32[512,768]{1,0:T(8,128)S(1)} %reshape.176, f32[768]{0:T(1024)S(1)} %copy-done.2, f32[768]{0:T(1024)S(1)} %copy-done.3, f32[512]{0:T(512)S(1)} %rsqrt.23, f32[512]{0:T(512)S(1)} %div.17), kind=kOutput, calls=%fused_computation.12 | convolution fusion | flops 304152576 | bytes 2566144 | tf_op jit(solution)/shard_map/dot_general | solution.py:62
  44.0 0.6 convolution_convert_fusion.1
  44.6 0.8 %reshape.173 = bf16[4,8,2,8,2,2,192]{6,5,4,3,2,1,0:T(2,128)(2,1)S(1)} reshape(bf16[512,768]{1,0:T(8,128)(2,1)S(1)} %convolution_convert_fusion.1) | data formatting | bytes 1572864 | tf_op jit(solution)/shard_map/reshape | solution.py:69
  45.4 0.2 slice.27
  45.6 0.7 copy.78
  46.4 1.9 %collective-permute-start.2 = (bf16[4,8,8,2,192]{4,2,3,1,0:T(8,128)(2,1)}, bf16[4,8,8,2,192]{4,2,3,1,0:T(8,128)(2,1)}, u32[]{:S(2)}, u32[]{:S(2)}) collective-permute-start(bf16[4,8,8,2,192]{4,2,3,1,0:T(8,128)(2,1)} %bitcast.40), channel_id=1, source_target_pairs={{0,7},{1,0},{2,1},{3,2},{4,3},{5,4},{6,5},{7,6},{8,15},{9,8},{10,9... | collective-permute-start | bytes 589832 | tf_op jit(solution)/shard_map/ppermute | solution.py:17
  48.2 0.2 copy.77
  48.6 0.9 %reshape.174 = bf16[4,16,4,1536]{3,1,2,0:T(8,128)(2,1)S(1)} reshape(bf16[4,8,2,2,2,8,192]{6,5,2,1,4,3,0:T(8,128)(2,1)S(1)} %bitcast.47) | data formatting | bytes 1572864 | tf_op jit(solution)/shard_map/reshape | solution.py:71
  49.6 0.5 copy.66
  50.1 4.2 %collective-permute-done.2 = bf16[4,8,8,2,192]{4,2,3,1,0:T(8,128)(2,1)} collective-permute-done((bf16[4,8,8,2,192]{4,2,3,1,0:T(8,128)(2,1)}, bf16[4,8,8,2,192]{4,2,3,1,0:T(8,128)(2,1)}, u32[]{:S(2)}, u32[]{:S(2)}) %collective-permute-start.2) | collective-permute-done | bytes 196640 | tf_op jit(solution)/shard_map/ppermute | solution.py:17
  54.3 1.5 %broadcast_in_dim_reshape.4 = bf16[4,16,1,1536]{3,2,1,0:T(2,128)(2,1)S(1)} reshape(bf16[4,8,2,8,192]{4,3,2,1,0:T(8,128)(2,1)} %bitcast.11) | data formatting | bytes 393216 | tf_op jit(solution)/shard_map/broadcast_in_dim;reshape | solution.py:75
  56.0 4.5 %collective-permute-start.3 = (bf16[4,3,4,1536]{3,2,1,0:T(4,128)(2,1)S(1)}, bf16[4,3,4,1536]{3,2,1,0:T(4,128)(2,1)S(1)}, u32[]{:S(2)}, u32[]{:S(2)}) collective-permute-start(bf16[4,3,4,1536]{3,2,1,0:T(4,128)(2,1)S(1)} %fusion.15), channel_id=1, source_target_pairs={{0,8},{8,16},{16,24},{1,9},{9,17},{17,25},{2,10},{10,18},{18,26},{... | collective-permute-start | bytes 442376 | tf_op jit(solution)/shard_map/ppermute | solution.py:12
  60.5 1.1 %broadcast_select_fusion.1 = bf16[4,8,2,3072]{3,2,1,0:T(2,128)(2,1)} fusion(bf16[4,8,2,3072]{3,2,1,0:T(2,128)(2,1)S(1)} %reshape.172, pred[8]{0:T(512)(128)(4,1)S(1)} %iota_compare_fusion.1), kind=kLoop, calls=%fused_computation.31 | loop fusion | flops 196608 | bytes 786440 | tf_op jit(solution)/shard_map/jit(_where)/select_n | solution.py:65
  61.6 0.9 %collective-permute-done.3 = bf16[4,3,4,1536]{3,2,1,0:T(4,128)(2,1)S(1)} collective-permute-done((bf16[4,3,4,1536]{3,2,1,0:T(4,128)(2,1)S(1)}, bf16[4,3,4,1536]{3,2,1,0:T(4,128)(2,1)S(1)}, u32[]{:S(2)}, u32[]{:S(2)}) %collective-permute-start.3) | collective-permute-done | bytes 147488 | tf_op jit(solution)/shard_map/ppermute | solution.py:12
  62.6 0.9 %maximum_maximum_fusion = bf16[4,19,4,1536]{3,2,1,0:T(4,128)(2,1)S(1)} fusion(bf16[4,16,1,1536]{3,2,1,0:T(2,128)(2,1)S(1)} %broadcast_in_dim_reshape.4, bf16[4,16,3,1536]{3,2,1,0:T(4,128)(2,1)S(1)} %copy.66, bf16[4,3,4,1536]{3,2,1,0:T(4,128)(2,1)S(1)} %collective-permute-done.3), kind=kLoop, calls=%fused_computation.14 | loop fusion | flops 2801664 | bytes 1867776 | tf_op jit(solution)/shard_map/concatenate | solution.py:78
  63.5 1.1 %gather_fusion.1 = bf16[14,4,4,1536]{3,2,1,0:T(4,128)(2,1)S(1)} fusion(bf16[4,19,4,1536]{3,2,1,0:T(4,128)(2,1)S(1)} %maximum_maximum_fusion, s32[1024]{0:T(1024)S(1)} %pad_clamp_fusion), kind=kCustom, calls=%fused_computation.1 | custom fusion | bytes 1376312 | tf_op jit(solution)/shard_map/jit(_take)/gather | solution.py:81
  64.6 0.8 %gather.15 = bf16[4,14,4,8,192]{4,3,2,0,1:T(8,128)(2,1)S(1)} reshape(bf16[4,14,4,1536]{3,2,0,1:T(4,128)(2,1)S(1)} %bitcast.44) | data formatting | bytes 1376256 | tf_op jit(solution)/shard_map/jit(_take)/gather | solution.py:81
  65.4 0.2 copy.59
  65.6 0.5 convert_reduce_fusion
  66.4 0.2 copy.62
  66.8 1.0 %fusion.1 = f32[4,14,4,8]{3,2,0,1:T(4,128)S(1)} fusion(f32[4,14,4,8]{3,2,0,1:T(4,128)S(1)} %copy.62, bf16[4,14,4,8,192]{4,3,2,0,1:T(8,128)(2,1)S(1)} %gather.15, pred[14]{0:T(512)(128)(4,1)S(1)} %compare_and_fusion), kind=kLoop, calls=%fused_computation.8 | loop fusion | flops 1718528 | bytes 702478 | tf_op jit(solution)/shard_map/reduce_sum | solution.py:22
  68.2 0.8 %gather.14 = bf16[1792,192]{1,0:T(8,128)(2,1)S(1)} reshape(bf16[4,14,4,1536]{3,2,1,0:T(4,128)(2,1)S(1)} %copy.59) | data formatting | bytes 1376256 | tf_op jit(solution)/shard_map/jit(_take)/gather | solution.py:81
  69.2 1.9 %convolution_convert_fusion = bf16[1792,192]{0,1:T(8,128)(2,1)S(1)} fusion(bf16[192,192]{1,0:T(8,128)(2,1)S(1)} %copy-done.1, f32[192]{0:T(256)S(1)} %copy-done.4, f32[192]{0:T(256)S(1)} %copy-done.5, f32[1792]{0:T(1024)S(1)} %rsqrt.25, f32[1792]{0:T(1024)S(1)} %div.20, bf16[1792,192]{1,0:T(8,128)(2,1)S(1)} %gather.14, pred[1792]{0:T(1024)(128)(4,1)S(1)} %broadcast_in_dim.76), kind=kOutput, calls=%fused_computation.2 | convolution fusion | flops 134873088 | bytes 1467648 | tf_op jit(solution)/shard_map/dot_general | solution.py:84
  71.1 0.5 copy.65
  71.6 0.8 %reshape.175 = bf16[4,14,4,1536]{3,2,1,0:T(4,128)(2,1)S(1)} reshape(bf16[1792,192]{1,0:T(8,128)(2,1)S(1)} %copy.65) | data formatting | bytes 1376256 | tf_op jit(solution)/shard_map/reshape | solution.py:87
  72.5 1.2 %broadcast_select_fusion.2 = bf16[4,14,4,1536]{3,2,1,0:T(4,128)(2,1)} fusion(bf16[4,14,4,1536]{3,2,1,0:T(4,128)(2,1)S(1)} %reshape.175, pred[14]{0:T(512)(128)(4,1)S(1)} %iota_compare_fusion), kind=kLoop, calls=%fused_computation.32 | loop fusion | flops 344064 | bytes 1376270 | tf_op jit(solution)/shard_map/jit(_where)/select_n | solution.py:89
  (35 shorter events, 1.9 us)
Async XLA Ops:
  0.6 43.4 %copy-start = (bf16[384,768]{1,0:T(8,128)(2,1)S(1)}, bf16[384,768]{1,0:T(8,128)(2,1)}, u32[]{:S(2)}) copy-start(bf16[384,768]{1,0:T(8,128)(2,1)} %param.16) | copy-start | bytes 1769476
  1.7 9.9 %collective-permute-start = (bf16[4,3,4,1536]{3,2,1,0:T(4,128)(2,1)S(1)}, bf16[4,3,4,1536]{3,2,1,0:T(4,128)(2,1)S(1)}, u32[]{:S(2)}, u32[]{:S(2)}) collective-permute-start(bf16[4,3,4,1536]{3,2,1,0:T(4,128)(2,1)S(1)} %slice.15), channel_id=1, source_target_pairs={{8,0},{16,8},{24,16},{9,1},{17,9},{25,17},{10,2},{18,10},{26,18},{... | collective-permute-start | bytes 442376 | tf_op jit(solution)/shard_map/ppermute | solution.py:12
  15.5 10.5 %collective-permute-start.1 = (bf16[4,16,1536]{2,1,0:T(8,128)(2,1)S(1)}, bf16[4,16,1536]{2,1,0:T(8,128)(2,1)S(1)}, u32[]{:S(2)}, u32[]{:S(2)}) collective-permute-start(bf16[4,16,1536]{2,1,0:T(8,128)(2,1)S(1)} %bitcast.48), channel_id=1, source_target_pairs={{0,1},{1,2},{2,3},{3,4},{4,5},{5,6},{6,7},{7,0},{8,9},{9,10},{10,1... | collective-permute-start | bytes 589832 | tf_op jit(solution)/shard_map/ppermute | solution.py:17
  39.0 3.2 %copy-start.2 = (f32[768]{0:T(1024)S(1)}, f32[768]{0:T(1024)}, u32[]{:S(2)}) copy-start(f32[768]{0:T(1024)} %param.14) | copy-start | bytes 9220
  39.0 3.2 %copy-start.3 = (f32[768]{0:T(1024)S(1)}, f32[768]{0:T(1024)}, u32[]{:S(2)}) copy-start(f32[768]{0:T(1024)} %param.13) | copy-start | bytes 9220
  46.4 7.9 %collective-permute-start.2 = (bf16[4,8,8,2,192]{4,2,3,1,0:T(8,128)(2,1)}, bf16[4,8,8,2,192]{4,2,3,1,0:T(8,128)(2,1)}, u32[]{:S(2)}, u32[]{:S(2)}) collective-permute-start(bf16[4,8,8,2,192]{4,2,3,1,0:T(8,128)(2,1)} %bitcast.40), channel_id=1, source_target_pairs={{0,7},{1,0},{2,1},{3,2},{4,3},{5,4},{6,5},{7,6},{8,15},{9,8},{10,9... | collective-permute-start | bytes 589832 | tf_op jit(solution)/shard_map/ppermute | solution.py:17
  56.0 6.6 %collective-permute-start.3 = (bf16[4,3,4,1536]{3,2,1,0:T(4,128)(2,1)S(1)}, bf16[4,3,4,1536]{3,2,1,0:T(4,128)(2,1)S(1)}, u32[]{:S(2)}, u32[]{:S(2)}) collective-permute-start(bf16[4,3,4,1536]{3,2,1,0:T(4,128)(2,1)S(1)} %fusion.15), channel_id=1, source_target_pairs={{0,8},{8,16},{16,24},{1,9},{9,17},{17,25},{2,10},{10,18},{18,26},{... | collective-permute-start | bytes 442376 | tf_op jit(solution)/shard_map/ppermute | solution.py:12
  66.6 2.6 %copy-start.1 = (bf16[192,192]{1,0:T(8,128)(2,1)S(1)}, bf16[192,192]{1,0:T(8,128)(2,1)}, u32[]{:S(2)}) copy-start(bf16[192,192]{1,0:T(8,128)(2,1)} %param.19) | copy-start | bytes 221188
  66.6 2.6 %copy-start.4 = (f32[192]{0:T(256)S(1)}, f32[192]{0:T(256)}, u32[]{:S(2)}) copy-start(f32[192]{0:T(256)} %param.18) | copy-start | bytes 2308
  66.6 2.6 %copy-start.5 = (f32[192]{0:T(256)S(1)}, f32[192]{0:T(256)}, u32[]{:S(2)}) copy-start(f32[192]{0:T(256)} %param.17) | copy-start | bytes 2308
where the time goes:
time: 74.1 us; the launch traced here: 73.7 us
  local copies, waits for them, and re-layouts  24.9 us (34%)
  other arithmetic  18 us (24%)
  waiting for transfers between devices  11.3 us (15%)
  starting transfers between devices  11.1 us (15%)
  between operations  4.24 us (6%)
  matrix products  4.17 us (6%)
    ppermute x2, waiting for transfers between devices, passed_along_2(): lax.ppermute(value, axis, [(i, (i + by) % size) for i in range(size)])  10.4 us
    convert_element_type x3, local copies, waits for them, and re-layouts, body(): pieces.astype(jnp.float32)  8.65 us
    ppermute x2, starting transfers between devices, passed_along(): lax.ppermute(value, axis, [(source, source + steps) for source in range(l...  6.42 us
    ppermute x2, starting transfers between devices, passed_along_2(): lax.ppermute(value, axis, [(i, (i + by) % size) for i in range(size)])  4.64 us
    reduce_sum x2, other arithmetic, layer_norm(): spread = jnp.mean(jnp.square(values - center), axis=-1, keepdims=True)  3.58 us
    reduce_sum x2, other arithmetic, layer_norm(): center = jnp.mean(values, axis=-1, keepdims=True)  2.98 us
    gather x4, local copies, waits for them, and re-layouts, body(): fine_rows = jnp.take(stacked_fine, spot, axis=1)  2.97 us
    convert_element_type x1, other arithmetic, body(): pieces.astype(jnp.float32)  1.92 us
  transfers between devices with their start and end apart: 4, of which 3 were waited for; matrix products, arithmetic and copies ran while one was open for 13% of the time, Pallas kernels for 0%

commit v1 on v0

v1 whole, which is shorter than its diff:
```python
import functools

import jax
import jax.numpy as jnp
from jax import lax
from jax.experimental import pallas as pl
from jax.experimental.pallas import tpu as pltpu
from jax.sharding import PartitionSpec as P

HALO = 3
LANES_OF_LEVELS = 4
MESH = pl.DeviceIdType.MESH


def norm(values, scale_vec, shift_vec):
    center = jnp.mean(values, axis=-1, keepdims=True)
    off = values - center
    spread = jnp.mean(off * off, axis=-1, keepdims=True)
    return off * lax.rsqrt(spread + 1e-05) * scale_vec + shift_vec


def kernel(
    n_lat,
    n_lon,
    in_b,
    out_b,
    t_ref,
    dw_hbm,
    uw_hbm,
    ow_hbm,
    dg_ref,
    db_ref,
    ug_ref,
    ub_ref,
    mo_ref,
    fo_ref,
    comb,
    west_in,
    east_in,
    top_in,
    bot_in,
    top_w,
    top_e,
    bot_w,
    bot_e,
    tail,
    tail_w,
    tail_e,
    nrm,
    dw,
    uw,
    ow,
    local_sem,
    send_sem,
    recv_sem,
):
    cols, slots, sub, lanes = t_ref.shape
    chan = lanes // LANES_OF_LEVELS
    total = slots + 2 * HALO
    rows = 2 * mo_ref.shape[0] + 4
    mid_lo, mid_hi = HALO, slots // 2
    lat = lax.axis_index("lat")
    lon = lax.axis_index("lon")
    east = {"lat": lat, "lon": lax.rem(lon + 1, n_lon)}
    west = {"lat": lat, "lon": lax.rem(lon + n_lon - 1, n_lon)}
    above = {"lat": jnp.maximum(lat - 1, 0), "lon": lon}
    below = {"lat": jnp.minimum(lat + 1, n_lat - 1), "lon": lon}
    has_above = lat > 0
    has_below = lat < n_lat - 1

    loads = [
        pltpu.make_async_copy(t_ref, comb.at[pl.ds(1, cols), pl.ds(HALO, slots)], local_sem.at[0]),
        pltpu.make_async_copy(dw_hbm, dw, local_sem.at[1]),
        pltpu.make_async_copy(uw_hbm, uw, local_sem.at[2]),
        pltpu.make_async_copy(ow_hbm, ow, local_sem.at[3]),
    ]
    for load in loads:
        load.start()

    barrier = pltpu.get_barrier_semaphore()
    pl.semaphore_signal(barrier, inc=1, device_id=east, device_id_type=MESH)
    pl.semaphore_signal(barrier, inc=1, device_id=west, device_id_type=MESH)

    @pl.when(has_above)
    def _():
        pl.semaphore_signal(barrier, inc=1, device_id=above, device_id_type=MESH)

    @pl.when(has_below)
    def _():
        pl.semaphore_signal(barrier, inc=1, device_id=below, device_id_type=MESH)

    pl.semaphore_wait(barrier, 2 + has_above.astype(jnp.int32) + has_below.astype(jnp.int32))

    def remote(src, dst, slot, device):
        return pltpu.make_async_remote_copy(
            src_ref=src,
            dst_ref=dst,
            send_sem=send_sem.at[slot],
            recv_sem=recv_sem.at[slot],
            device_id=device,
            device_id_type=MESH,
        )

    spans = [(0, mid_lo), (mid_hi, slots), (mid_lo, mid_hi)]
    to_east, to_west = [], []
    for i, (lo, hi) in enumerate(spans):
        span = pl.ds(lo, hi - lo)
        to_east.append(remote(t_ref.at[cols - 1, span], west_in.at[span], i, east))
        to_west.append(remote(t_ref.at[0, span], east_in.at[span], 3 + i, west))
    up = remote(t_ref.at[:, pl.ds(0, HALO)], bot_in, 6, above)
    down = remote(tail, top_in, 7, below)
    head = pl.ds(0, HALO)
    up_w = remote(west_in.at[head], bot_w, 8, above)
    up_e = remote(east_in.at[head], bot_e, 9, above)
    down_w = remote(tail_w, top_w, 10, below)
    down_e = remote(tail_e, top_e, 11, below)

    for i in range(2):
        to_east[i].start()
        to_west[i].start()

    @pl.when(has_above)
    def _():
        up.start()

    to_east[2].start()
    to_west[2].start()

    start_in = in_b[lat]
    end_in = in_b[lat + 1]
    count = end_in - start_in
    shift = 2 * out_b[lat] - start_in
    past = count - shift + 4

    loads[0].wait()
    for x in range(cols):
        for i in range(HALO):
            tail[x, i] = comb[1 + x, count + i]

    @pl.when(has_below)
    def _():
        down.start()

    for load in loads[1:]:
        load.wait()

    def place(r):
        inside = jnp.maximum(r + shift - 1, 0)
        outside = jnp.minimum(HALO + slots + r - past, total - 1)
        return jnp.where(r < past, inside, outside)

    spots = [place(r) for r in range(rows)]

    dg = dg_ref[...]
    db = db_ref[...]
    ug = ug_ref[...]
    ub = ub_ref[...]

    def compute(j, ms):
        nm = len(ms)
        size = LANES_OF_LEVELS * nm * sub
        for k in range(0, nm, 2):
            blocks = []
            for c in range(2):
                for a in range(2):
                    blocks.append(
                        jnp.concatenate(
                            [comb[2 * j + c, spots[2 * m + a]].astype(jnp.float32) for m in ms[k : k + 2]],
                            axis=0,
                        )
                    )
            for level in range(LANES_OF_LEVELS):
                cut = slice(level * chan, (level + 1) * chan)
                pieces = jnp.concatenate([block[:, cut] for block in blocks], axis=1)
                at = (level * nm + k) * sub
                nrm[at : at + 2 * sub, :] = norm(pieces, dg, db).astype(jnp.bfloat16)
        wide = jnp.dot(nrm[0:size, :], dw[...], preferred_element_type=jnp.float32)
        coarse = wide.astype(jnp.bfloat16)
        if j < 2:
            for i, m in enumerate(ms):
                if m < 2:
                    continue
                for level in range(LANES_OF_LEVELS):
                    at = (level * nm + i) * sub
                    mo_ref[m - 2, j, :, level * 2 * chan : (level + 1) * 2 * chan] = wide[
                        at : at + sub
                    ].astype(jnp.bfloat16)
        for c, x in (((1, 0),), ((0, 1), (1, 2)), ((0, 3),))[j]:
            spread = jnp.dot(
                coarse, uw[:, c * 2 * chan : (c + 1) * 2 * chan], preferred_element_type=jnp.float32
            ).astype(jnp.bfloat16)
            spread = spread.astype(jnp.float32)
            for a in range(2):
                half = norm(spread[:, a * chan : (a + 1) * chan], ug, ub).astype(jnp.bfloat16)
                done = jnp.dot(half, ow[...], preferred_element_type=jnp.float32)
                for i, m in enumerate(ms):
                    fo_ref[2 * m + a, x] = jnp.concatenate(
                        [
                            done[(level * nm + i) * sub : (level * nm + i + 1) * sub]
                            for level in range(LANES_OF_LEVELS)
                        ],
                        axis=1,
                    ).astype(jnp.bfloat16)

    own = pl.ds(1, cols)

    @pl.when(has_above)
    def _():
        down.wait_recv()

    @pl.when(has_below)
    def _():
        up.wait_recv()
        comb[own, HALO + slots : total] = bot_in[...]

    @pl.when(jnp.logical_not(has_below))
    def _():
        comb[:, HALO + slots : total] = jnp.zeros((cols + 2, HALO, sub, lanes), jnp.bfloat16)

    @pl.when(has_above)
    def _():
        comb[own, 0:HALO] = top_in[...]

    @pl.when(jnp.logical_not(has_above))
    def _():
        comb[:, 0:HALO] = jnp.zeros((cols + 2, HALO, sub, lanes), jnp.bfloat16)

    merged_rows = rows // 2
    compute(1, list(range(merged_rows)))

    for i in range(2):
        lo, hi = spans[i]
        to_east[i].wait_recv()
        comb[0, HALO + lo : HALO + hi] = west_in[lo:hi]
        to_west[i].wait_recv()
        comb[cols + 1, HALO + lo : HALO + hi] = east_in[lo:hi]
    for i in range(HALO):
        tail_w[i] = comb[0, count + i]
        tail_e[i] = comb[cols + 1, count + i]

    @pl.when(has_above)
    def _():
        up_w.start()
        up_e.start()

    @pl.when(has_below)
    def _():
        down_w.start()
        down_e.start()

    lo, hi = spans[2]
    to_east[2].wait_recv()
    comb[0, HALO + lo : HALO + hi] = west_in[lo:hi]
    to_west[2].wait_recv()
    comb[cols + 1, HALO + lo : HALO + hi] = east_in[lo:hi]

    @pl.when(has_above)
    def _():
        down_w.wait_recv()
        comb[0, 0:HALO] = top_w[...]
        down_e.wait_recv()
        comb[cols + 1, 0:HALO] = top_e[...]

    @pl.when(has_below)
    def _():
        up_w.wait_recv()
        comb[0, HALO + slots : total] = bot_w[...]
        up_e.wait_recv()
        comb[cols + 1, HALO + slots : total] = bot_e[...]

    compute(0, list(range(merged_rows)))
    compute(2, list(range(merged_rows)))

    for copy in to_east + to_west:
        copy.wait_send()

    @pl.when(has_above)
    def _():
        up.wait_send()
        up_w.wait_send()
        up_e.wait_send()

    @pl.when(has_below)
    def _():
        down.wait_send()
        down_w.wait_send()
        down_e.wait_send()


def body(
    tokens,
    in_bounds,
    out_bounds,
    down_gain,
    down_bias,
    down_weight,
    up_weight,
    up_gain,
    up_bias,
    out_weight,
):
    members, slots, cols, packed = tokens.shape
    chan = down_weight.shape[0] // 4
    halves = packed // (chan * LANES_OF_LEVELS)
    lanes = chan * LANES_OF_LEVELS
    sub = halves * members
    merged_slots = slots // 2 + 1
    half_cols = cols // 2
    rows = 2 * merged_slots + 4
    total = slots + 2 * HALO
    bf16 = jnp.bfloat16
    n_lat = lax.axis_size("lat")
    n_lon = lax.axis_size("lon")
    grid_tokens = tokens.reshape(members, slots, cols, halves, lanes)
    grid_tokens = grid_tokens.transpose(2, 1, 3, 0, 4).reshape(cols, slots, sub, lanes)
    smem = pl.BlockSpec(memory_space=pltpu.SMEM)
    vmem = pl.BlockSpec(memory_space=pltpu.VMEM)
    hbm = pl.BlockSpec(memory_space=pl.ANY)
    column = pltpu.VMEM((slots, sub, lanes), bf16)
    patch = pltpu.VMEM((cols, HALO, sub, lanes), bf16)
    corner = pltpu.VMEM((HALO, sub, lanes), bf16)
    merged_raw, fine_raw = pl.pallas_call(
        functools.partial(kernel, n_lat, n_lon),
        out_shape=(
            jax.ShapeDtypeStruct((merged_slots, half_cols, sub, 2 * lanes), bf16),
            jax.ShapeDtypeStruct((rows, cols, sub, lanes), bf16),
        ),
        in_specs=[smem, smem, hbm, hbm, hbm, hbm, vmem, vmem, vmem, vmem],
        out_specs=(vmem, vmem),
        scratch_shapes=[
            pltpu.VMEM((cols + 2, total, sub, lanes), bf16),
            column,
            column,
            patch,
            patch,
            corner,
            corner,
            corner,
            corner,
            patch,
            corner,
            corner,
            pltpu.VMEM((LANES_OF_LEVELS * rows // 2 * sub, 4 * chan), bf16),
            pltpu.VMEM(down_weight.shape, bf16),
            pltpu.VMEM(up_weight.shape, bf16),
            pltpu.VMEM(out_weight.shape, bf16),
            pltpu.SemaphoreType.DMA((4,)),
            pltpu.SemaphoreType.DMA((12,)),
            pltpu.SemaphoreType.DMA((12,)),
        ],
        compiler_params=pltpu.CompilerParams(collective_id=0, has_side_effects=True),
    )(
        in_bounds,
        out_bounds,
        grid_tokens,
        down_weight,
        up_weight,
        out_weight,
        down_gain[None],
        down_bias[None],
        up_gain[None],
        up_bias[None],
    )
    band = lax.axis_index("lat")
    count_in = in_bounds[band + 1] - in_bounds[band]
    count_out = out_bounds[band + 1] - out_bounds[band]
    shift = 2 * out_bounds[band] - in_bounds[band]
    zero = jnp.zeros((), bf16)
    merged = merged_raw.reshape(merged_slots, half_cols, halves, members, 2 * lanes)
    merged = merged.transpose(3, 0, 1, 2, 4).reshape(members, merged_slots, half_cols, 2 * packed)
    merged_live = jnp.arange(merged_slots, dtype=jnp.int32) < count_out
    merged = jnp.where(merged_live[None, :, None, None], merged, zero)
    fine = lax.dynamic_slice_in_dim(fine_raw, 4 - shift, slots, 0)
    fine = fine.reshape(slots, cols, halves, members, lanes).transpose(3, 0, 1, 2, 4)
    fine = fine.reshape(members, slots, cols, packed)
    fine_live = jnp.arange(slots, dtype=jnp.int32) < count_in
    return merged, jnp.where(fine_live[None, :, None, None], fine, zero)


def solution(mesh):
    return jax.shard_map(
        body,
        mesh=mesh,
        in_specs=(P(None, "lat", "lon", None), P(), P(), P(), P(), P(), P(), P(), P(), P()),
        out_specs=(P(None, "lat", "lon", None), P(None, "lat", "lon", None)),
        check_vma=False,
    )
```

time: 74.1 us -> 39.2 us (0.53)
  Pallas kernels: 0 us -> 23.6 us
  local copies, waits for them, and re-layouts: 24.9 us -> 8.48 us
  other arithmetic: 18 us -> 2.35 us
  waiting for transfers between devices: 11.3 us -> 0 us
  starting transfers between devices: 11.1 us -> 0 us
  matrix products: 4.17 us -> 0 us
    pallas_call x0 -> x1, Pallas kernels: none -> 23.6 us  [body(): pl.pallas_call(functools.partial(kernel, n_lat, n_lon), out_shape=(jax.Sh...]
    ppermute x4 -> x0, waiting for transfers between devices: 11.3 us -> none  [the longest x2 10.4 us: passed_along_2(): lax.ppermute(value, axis, [(i, (i + by) % size) for i in range(size)])]
    ppermute x4 -> x0, starting transfers between devices: 11.1 us -> none  [the longest x2 6.42 us: passed_along(): lax.ppermute(value, axis, [(source, source + steps) for source in range(l...]
    convert_element_type x4 -> x0, local copies, waits for them, and re-layouts: 9.17 us -> none  [the longest x3 8.65 us: body(): pieces.astype(jnp.float32)]
    reduce_sum x4 -> x0, other arithmetic: 6.56 us -> none  [the longest x2 3.58 us: layer_norm(): spread = jnp.mean(jnp.square(values - center), axis=-1, keepdims=True)]
    gather x5 -> x0, local copies, waits for them, and re-layouts: 4.19 us -> none  [the longest x4 2.97 us: body(): fine_rows = jnp.take(stacked_fine, spot, axis=1)]
    dot_general x3 -> x0, matrix products: 4.17 us -> none  [the longest x1 1.87 us: body(): jnp.dot(renormed.reshape(-1, channels), out_weight, preferred_element_typ...]
    concatenate x3 -> x0, other arithmetic: 2.69 us -> none  [the longest x1 1.65 us: body(): stacked = jnp.concatenate([tokens, from_below], axis=1)]
  transfers between devices with their start and end apart: 4 -> 0, of which waited for: 3 -> 0; matrix products, arithmetic and copies ran while one was open for 13% -> 0% of each run, Pallas kernels for 0% -> 0%
where the time goes in v1:
time: 39.2 us; the launch traced here: 38.9 us
  Pallas kernels  23.6 us (60%)
  local copies, waits for them, and re-layouts  8.48 us (22%)
  between operations  4.47 us (11%)
  other arithmetic  2.35 us (6%)
    pallas_call x1, Pallas kernels, body(): pl.pallas_call(functools.partial(kernel, n_lat, n_lon), out_shape=(jax.Sh...  23.6 us
    reshape x2, local copies, waits for them, and re-layouts, body(): grid_tokens = tokens.reshape(members, slots, cols, halves, lanes)  2.51 us
    select_n x1, other arithmetic, body(): return (merged, jnp.where(fine_live[None, :, None, None], fine, zero))  1.2 us
    select_n x1, other arithmetic, body(): merged = jnp.where(merged_live[None, :, None, None], merged, zero)  1.14 us
    reshape x1, local copies, waits for them, and re-layouts, body(): merged_raw.reshape(merged_slots, half_cols, halves, members, 2 * lanes)  1.09 us
    reshape x1, local copies, waits for them, and re-layouts, body(): grid_tokens.transpose(2, 1, 3, 0, 4).reshape(cols, slots, sub, lanes)  1.01 us

profile of v1, /device:TPU:1, one launch (start us, length us, event | category | flops | bytes accessed | tf_op | source)
XLA Modules:
  0.0 38.9 jit_solution(8275746322464798659)
XLA Ops:
  0.6 2.2 %reshape.39 = bf16[4,14,4,2,768]{4,3,2,1,0:T(2,128)(2,1)S(1)} reshape(bf16[4,14,4,1536]{3,2,1,0:T(4,128)(2,1)} %param.10) | data formatting | bytes 1376256 | tf_op jit(solution)/shard_map/reshape | solution.py:314
  2.8 0.4 copy.22
  3.2 0.0 copy-start.3
  3.2 1.0 %reshape.40.t_ref = bf16[4,14,8,768]{3,2,1,0:T(8,128)(2,1)} reshape(bf16[4,14,2,4,768]{4,3,2,1,0:T(4,128)(2,1)S(1)} %bitcast.15) | data formatting | bytes 1376256 | tf_op jit(solution)/shard_map/reshape | solution.py:315
  4.2 0.0 copy-done.3
  4.2 0.0 copy-start.4
  4.2 0.6 %broadcast_in_dim.39.dg_ref = f32[1,768]{1,0:T(1,128)} reshape(f32[768]{0:T(1024)S(1)} %copy-done.3) | data formatting | bytes 6144 | tf_op jit(solution)/shard_map/broadcast_in_dim | solution.py:359
  4.8 0.1 copy-done.4
  4.9 0.6 %broadcast_in_dim.40.db_ref = f32[1,768]{1,0:T(1,128)} reshape(f32[768]{0:T(1024)S(1)} %copy-done.4) | data formatting | bytes 6144 | tf_op jit(solution)/shard_map/broadcast_in_dim | solution.py:360
  5.4 23.6 %shard_map.113 = (bf16[8,2,8,1536]{3,2,1,0:T(8,128)(2,1)}, bf16[20,4,8,768]{3,2,1,0:T(8,128)(2,1)}) custom-call(s32[5]{0:T(128)} %in_b.1, s32[5]{0:T(128)} %out_b.1, bf16[4,14,8,768]{3,2,1,0:T(8,128)(2,1)} %reshape.40.t_ref, bf16[768,384]{1,0:T(8,128)(2,1)} %dw_hbm.1, bf16[384,768]{1,0:T(8,128)(2,1)} %uw_hbm.1, bf16[192,192]{1,0:T(8,128)(2,1)} %ow_hbm.1, ...), custom_call_target="tpu_custom_call" | custom-call | tf_op jit(solution)/shard_map/pallas_call | solution.py:322
  29.0 1.1 %reshape.41 = bf16[8,2,2,4,1536]{4,3,2,1,0:T(4,128)(2,1)S(1)} reshape(bf16[8,2,8,1536]{3,2,1,0:T(8,128)(2,1)} %get-tuple-element.4) | data formatting | bytes 786432 | tf_op jit(solution)/shard_map/reshape | solution.py:369
  30.1 0.0 copy-start.1
  30.2 0.0 copy-start.2
  30.2 0.3 copy.18
  30.5 0.0 copy-start
  30.5 0.2 reshape.42
  30.7 0.0 copy-done.1
  30.8 0.0 copy-done.2
  30.8 0.6 %fusion = (s32[1]{0:T(128)}, s32[1]{0:T(128)}, s32[1]{0:T(128)}, s32[1]{0:T(128)}) fusion(s32[5]{0:T(128)S(1)} %copy-done.1, s32[]{:T(128)S(6)} %select_n.21, s32[]{:T(128)S(6)} %select_n.22, s32[5]{0:T(128)S(1)} %copy-done.2), kind=kLoop, calls=%fused_computation.6 | loop fusion | bytes 40 | tf_op jit(solution)/shard_map/dynamic_slice | solution.py:365
  32.7 1.1 %broadcast_select_fusion = bf16[4,8,2,3072]{3,2,1,0:T(2,128)(2,1)} fusion(bf16[4,8,2,3072]{3,2,1,0:T(2,128)(2,1)S(1)} %reshape.42, pred[8]{0:T(512)(128)(4,1)S(1)} %iota_compare_fusion.1), kind=kLoop, calls=%fused_computation | loop fusion | flops 196608 | bytes 786440 | tf_op jit(solution)/shard_map/jit(_where)/select_n | solution.py:372
  35.0 0.0 copy-done
  35.1 0.1 constant_dynamic-slice_fusion
  35.1 0.3 copy.19
  35.4 0.5 %copy.20 = bf16[4,14,4,2,768]{4,3,2,1,0:T(2,128)(2,1)S(1)} copy(bf16[4,14,4,2,768]{4,2,0,3,1:T(4,128)(2,1)S(1)} %bitcast.16) | data formatting | bytes 1376256 | tf_op jit(solution)/shard_map/transpose | solution.py:374
  36.0 0.4 %reshape.44 = bf16[4,14,4,1536]{3,2,1,0:T(4,128)(2,1)S(1)} reshape(bf16[4,14,4,2,768]{4,3,2,1,0:T(2,128)(2,1)S(1)} %copy.20) | data formatting | bytes 1376256 | tf_op jit(solution)/shard_map/reshape | solution.py:375
  37.7 1.2 %broadcast_select_fusion.1 = bf16[4,14,4,1536]{3,2,1,0:T(4,128)(2,1)} fusion(bf16[4,14,4,1536]{3,2,1,0:T(4,128)(2,1)S(1)} %reshape.44, pred[14]{0:T(512)(128)(4,1)S(1)} %iota_compare_fusion), kind=kLoop, calls=%fused_computation.2 | loop fusion | flops 344064 | bytes 1376270 | tf_op jit(solution)/shard_map/jit(_where)/select_n | solution.py:377
  (2 shorter events, 0.0 us)
Async XLA Ops:
  3.2 1.0 %copy-start.3 = (f32[768]{0:T(1024)S(1)}, f32[768]{0:T(1024)}, u32[]{:S(2)}) copy-start(f32[768]{0:T(1024)} %param.13) | copy-start | bytes 9220
  4.2 0.7 %copy-start.4 = (f32[768]{0:T(1024)S(1)}, f32[768]{0:T(1024)}, u32[]{:S(2)}) copy-start(f32[768]{0:T(1024)} %param.14) | copy-start | bytes 9220
  30.1 0.7 %copy-start.1 = (s32[5]{0:T(128)S(1)}, s32[5]{0:T(128)}, u32[]{:S(2)}) copy-start(s32[5]{0:T(128)} %in_b.1) | copy-start | bytes 64
  30.2 0.7 %copy-start.2 = (s32[5]{0:T(128)S(1)}, s32[5]{0:T(128)}, u32[]{:S(2)}) copy-start(s32[5]{0:T(128)} %out_b.1) | copy-start | bytes 64
  30.5 4.6 %copy-start = (bf16[20,4,8,768]{3,2,1,0:T(8,128)(2,1)S(1)}, bf16[20,4,8,768]{3,2,1,0:T(8,128)(2,1)}, u32[]{:S(2)}) copy-start(bf16[20,4,8,768]{3,2,1,0:T(8,128)(2,1)} %get-tuple-element.5) | copy-start | bytes 2949124

commit v2 on v1

--- a/solution.py
+++ b/solution.py
@@ -9,6 +9,7 @@
 
 HALO = 3
 LANES_OF_LEVELS = 4
+TILE = 128
 MESH = pl.DeviceIdType.MESH
 
 
@@ -47,6 +48,9 @@
     tail_w,
     tail_e,
     nrm,
+    turn_in,
+    turn_merged,
+    turn_fine,
     dw,
     uw,
     ow,
@@ -54,10 +58,14 @@
     send_sem,
     recv_sem,
 ):
-    cols, slots, sub, lanes = t_ref.shape
+    members, slots, cols, packed = t_ref.shape
+    merged_slots = mo_ref.shape[1]
+    _, _, sub, lanes = comb.shape
+    halves = sub // members
     chan = lanes // LANES_OF_LEVELS
+    tiles = lanes // TILE
     total = slots + 2 * HALO
-    rows = 2 * mo_ref.shape[0] + 4
+    rows = 2 * merged_slots + 4
     mid_lo, mid_hi = HALO, slots // 2
     lat = lax.axis_index("lat")
     lon = lax.axis_index("lon")
@@ -69,10 +77,9 @@
     has_below = lat < n_lat - 1
 
     loads = [
-        pltpu.make_async_copy(t_ref, comb.at[pl.ds(1, cols), pl.ds(HALO, slots)], local_sem.at[0]),
-        pltpu.make_async_copy(dw_hbm, dw, local_sem.at[1]),
-        pltpu.make_async_copy(uw_hbm, uw, local_sem.at[2]),
-        pltpu.make_async_copy(ow_hbm, ow, local_sem.at[3]),
+        pltpu.make_async_copy(dw_hbm, dw, local_sem.at[0]),
+        pltpu.make_async_copy(uw_hbm, uw, local_sem.at[1]),
+        pltpu.make_async_copy(ow_hbm, ow, local_sem.at[2]),
     ]
     for load in loads:
         load.start()
@@ -88,6 +95,25 @@
     @pl.when(has_below)
     def _():
         pl.semaphore_signal(barrier, inc=1, device_id=below, device_id_type=MESH)
+
+    for r in range(slots):
+        for member in range(members):
+            row = t_ref[member, r].astype(jnp.float32)
+            for half in range(halves):
+                at = (half * members + member) * cols
+                for t in range(tiles):
+                    lane = half * lanes + t * TILE
+                    turn_in[r, t, at : at + cols, :] = row[:, lane : lane + TILE]
+
+    def take_column(x):
+        for r in range(slots):
+            for t in range(tiles):
+                comb[1 + x, HALO + r, :, t * TILE : (t + 1) * TILE] = turn_in[
+                    r, t, pl.ds(x, sub, stride=cols), :
+                ].astype(jnp.bfloat16)
+
+    take_column(cols - 1)
+    take_column(0)
 
     pl.semaphore_wait(barrier, 2 + has_above.astype(jnp.int32) + has_below.astype(jnp.int32))
 
@@ -105,9 +131,10 @@
     to_east, to_west = [], []
     for i, (lo, hi) in enumerate(spans):
         span = pl.ds(lo, hi - lo)
-        to_east.append(remote(t_ref.at[cols - 1, span], west_in.at[span], i, east))
-        to_west.append(remote(t_ref.at[0, span], east_in.at[span], 3 + i, west))
-    up = remote(t_ref.at[:, pl.ds(0, HALO)], bot_in, 6, above)
+        held = pl.ds(HALO + lo, hi - lo)
+        to_east.append(remote(comb.at[cols, held], west_in.at[span], i, east))
+        to_west.append(remote(comb.at[1, held], east_in.at[span], 3 + i, west))
+    up = remote(comb.at[pl.ds(1, cols), pl.ds(HALO, HALO)], bot_in, 6, above)
     down = remote(tail, top_in, 7, below)
     head = pl.ds(0, HALO)
     up_w = remote(west_in.at[head], bot_w, 8, above)
@@ -115,16 +142,16 @@
     down_w = remote(tail_w, top_w, 10, below)
     down_e = remote(tail_e, top_e, 11, below)
 
-    for i in range(2):
+    for i in range(3):
         to_east[i].start()
         to_west[i].start()
 
+    for x in range(1, cols - 1):
+        take_column(x)
+
     @pl.when(has_above)
     def _():
         up.start()
-
-    to_east[2].start()
-    to_west[2].start()
 
     start_in = in_b[lat]
     end_in = in_b[lat + 1]
@@ -132,7 +159,6 @@
     shift = 2 * out_b[lat] - start_in
     past = count - shift + 4
 
-    loads[0].wait()
     for x in range(cols):
         for i in range(HALO):
             tail[x, i] = comb[1 + x, count + i]
@@ -141,7 +167,7 @@
     def _():
         down.start()
 
-    for load in loads[1:]:
+    for load in loads:
         load.wait()
 
     def place(r):
@@ -151,10 +177,10 @@
 
     spots = [place(r) for r in range(rows)]
 
-    dg = dg_ref[...]
-    db = db_ref[...]
-    ug = ug_ref[...]
-    ub = ub_ref[...]
+    dg = dg_ref[...][None]
+    db = db_ref[...][None]
+    ug = ug_ref[...][None]
+    ub = ub_ref[...][None]
 
     def compute(j, ms):
         nm = len(ms)
@@ -182,9 +208,10 @@
                     continue
                 for level in range(LANES_OF_LEVELS):
                     at = (level * nm + i) * sub
-                    mo_ref[m - 2, j, :, level * 2 * chan : (level + 1) * 2 * chan] = wide[
-                        at : at + sub
-                    ].astype(jnp.bfloat16)
+                    for t in range(2 * chan // TILE):
+                        turn_merged[
+                            m - 2, level * 2 * chan // TILE + t, pl.ds(j, sub, stride=cols // 2), :
+                        ] = wide[at : at + sub, t * TILE : (t + 1) * TILE]
         for c, x in (((1, 0),), ((0, 1), (1, 2)), ((0, 3),))[j]:
             spread = jnp.dot(
                 coarse, uw[:, c * 2 * chan : (c + 1) * 2 * chan], preferred_element_type=jnp.float32
@@ -194,13 +221,17 @@
                 half = norm(spread[:, a * chan : (a + 1) * chan], ug, ub).astype(jnp.bfloat16)
                 done = jnp.dot(half, ow[...], preferred_element_type=jnp.float32)
                 for i, m in enumerate(ms):
-                    fo_ref[2 * m + a, x] = jnp.concatenate(
+                    line = jnp.concatenate(
                         [
                             done[(level * nm + i) * sub : (level * nm + i + 1) * sub]
                             for level in range(LANES_OF_LEVELS)
                         ],
                         axis=1,
-                    ).astype(jnp.bfloat16)
+                    )
+                    for t in range(tiles):
+                        turn_fine[2 * m + a, t, pl.ds(x, sub, stride=cols), :] = line[
+                            :, t * TILE : (t + 1) * TILE
+                        ]
 
     own = pl.ds(1, cols)
 
@@ -268,8 +299,22 @@
         up_e.wait_recv()
         comb[cols + 1, HALO + slots : total] = bot_e[...]
 
+    def put_out(value, live, slot, out_ref, width, span):
+        value = jnp.where(live, value, 0.0).astype(jnp.bfloat16)
+        for half in range(halves):
+            for member in range(members):
+                at = (half * members + member) * width
+                out_ref[member, slot, :, half * span : (half + 1) * span] = jnp.concatenate(
+                    [value[t, at : at + width] for t in range(span // TILE)], axis=1
+                )
+
     compute(0, list(range(merged_rows)))
+    count_out = out_b[lat + 1] - out_b[lat]
+    for m in range(merged_slots):
+        put_out(turn_merged[m], m < count_out, m, mo_ref, cols // 2, 2 * lanes)
     compute(2, list(range(merged_rows)))
+    for k in range(slots):
+        put_out(turn_fine[4 - shift + k], k < count, k, fo_ref, cols, lanes)
 
     for copy in to_east + to_west:
         copy.wait_send()
@@ -311,21 +356,19 @@
     bf16 = jnp.bfloat16
     n_lat = lax.axis_size("lat")
     n_lon = lax.axis_size("lon")
-    grid_tokens = tokens.reshape(members, slots, cols, halves, lanes)
-    grid_tokens = grid_tokens.transpose(2, 1, 3, 0, 4).reshape(cols, slots, sub, lanes)
     smem = pl.BlockSpec(memory_space=pltpu.SMEM)
     vmem = pl.BlockSpec(memory_space=pltpu.VMEM)
     hbm = pl.BlockSpec(memory_space=pl.ANY)
     column = pltpu.VMEM((slots, sub, lanes), bf16)
     patch = pltpu.VMEM((cols, HALO, sub, lanes), bf16)
     corner = pltpu.VMEM((HALO, sub, lanes), bf16)
-    merged_raw, fine_raw = pl.pallas_call(
+    return pl.pallas_call(
         functools.partial(kernel, n_lat, n_lon),
         out_shape=(
-            jax.ShapeDtypeStruct((merged_slots, half_cols, sub, 2 * lanes), bf16),
-            jax.ShapeDtypeStruct((rows, cols, sub, lanes), bf16),
+            jax.ShapeDtypeStruct((members, merged_slots, half_cols, 2 * packed), bf16),
+            jax.ShapeDtypeStruct(tokens.shape, bf16),
         ),
-        in_specs=[smem, smem, hbm, hbm, hbm, hbm, vmem, vmem, vmem, vmem],
+        in_specs=[smem, smem, vmem, hbm, hbm, hbm, vmem, vmem, vmem, vmem],
         out_specs=(vmem, vmem),
         scratch_shapes=[
             pltpu.VMEM((cols + 2, total, sub, lanes), bf16),
@@ -341,10 +384,13 @@
             corner,
             corner,
             pltpu.VMEM((LANES_OF_LEVELS * rows // 2 * sub, 4 * chan), bf16),
+            pltpu.VMEM((slots, lanes // TILE, sub * cols, TILE), jnp.float32),
+            pltpu.VMEM((merged_slots, 2 * lanes // TILE, sub * half_cols, TILE), jnp.float32),
+            pltpu.VMEM((rows, lanes // TILE, sub * cols, TILE), jnp.float32),
             pltpu.VMEM(down_weight.shape, bf16),
             pltpu.VMEM(up_weight.shape, bf16),
             pltpu.VMEM(out_weight.shape, bf16),
-            pltpu.SemaphoreType.DMA((4,)),
+            pltpu.SemaphoreType.DMA((3,)),
             pltpu.SemaphoreType.DMA((12,)),
             pltpu.SemaphoreType.DMA((12,)),
         ],
@@ -352,29 +398,15 @@
     )(
         in_bounds,
         out_bounds,
-        grid_tokens,
+        tokens,
         down_weight,
         up_weight,
         out_weight,
-        down_gain[None],
-        down_bias[None],
-        up_gain[None],
-        up_bias[None],
+        down_gain,
+        down_bias,
+        up_gain,
+        up_bias,
     )
-    band = lax.axis_index("lat")
-    count_in = in_bounds[band + 1] - in_bounds[band]
-    count_out = out_bounds[band + 1] - out_bounds[band]
-    shift = 2 * out_bounds[band] - in_bounds[band]
-    zero = jnp.zeros((), bf16)
-    merged = merged_raw.reshape(merged_slots, half_cols, halves, members, 2 * lanes)
-    merged = merged.transpose(3, 0, 1, 2, 4).reshape(members, merged_slots, half_cols, 2 * packed)
-    merged_live = jnp.arange(merged_slots, dtype=jnp.int32) < count_out
-    merged = jnp.where(merged_live[None, :, None, None], merged, zero)
-    fine = lax.dynamic_slice_in_dim(fine_raw, 4 - shift, slots, 0)
-    fine = fine.reshape(slots, cols, halves, members, lanes).transpose(3, 0, 1, 2, 4)
-    fine = fine.reshape(members, slots, cols, packed)
-    fine_live = jnp.arange(slots, dtype=jnp.int32) < count_in
-    return merged, jnp.where(fine_live[None, :, None, None], fine, zero)
 
 
 def solution(mesh):

time: 39.2 us -> 27.5 us (0.70)
  local copies, waits for them, and re-layouts: 8.48 us -> 2.93 us
  between operations: 4.47 us -> 0.65 us
  other arithmetic: 2.35 us -> 0 us
    reshape x6 -> x0, local copies, waits for them, and re-layouts: 5.29 us -> none  [the longest x2 2.51 us: body(): grid_tokens = tokens.reshape(members, slots, cols, halves, lanes)]
    unnamed x10 -> x4, local copies, waits for them, and re-layouts: 0.19 us -> 2.93 us
    select_n x2 -> x0, other arithmetic: 2.34 us -> none  [the longest x1 1.2 us: body(): return (merged, jnp.where(fine_live[None, :, None, None], fine, zero))]
    broadcast_in_dim x2 -> x0, local copies, waits for them, and re-layouts: 1.16 us -> none  [the longest x1 0.58 us: body(): down_gain[None]]
    dynamic_slice x3 -> x0, local copies, waits for them, and re-layouts: 1 us -> none  [the longest x1 0.65 us: body(): count_in = in_bounds[band + 1] - in_bounds[band]]
    transpose x2 -> x0, local copies, waits for them, and re-layouts: 0.84 us -> none  [the longest x1 0.53 us: body(): fine.reshape(slots, cols, halves, members, lanes).transpose(3, 0, 1, 2, 4)]
where the time goes in v2:
time: 27.5 us; the launch traced here: 27.3 us
  Pallas kernels  23.8 us (87%)
  local copies, waits for them, and re-layouts  2.93 us (11%)
  between operations  0.65 us (2%)
    pallas_call x1, Pallas kernels, body(): pl.pallas_call(functools.partial(kernel, n_lat, n_lon), out_shape=(jax.Sh...  23.8 us
    unnamed x4, local copies, waits for them, and re-layouts  2.93 us

profile of v2, /device:TPU:1, one launch (start us, length us, event | category | flops | bytes accessed | tf_op | source)
XLA Modules:
  0.0 27.3 jit_solution(3620627070311629431)
XLA Ops:
  0.6 23.8 %shard_map.113 = (bf16[4,8,2,3072]{3,2,1,0:T(2,128)(2,1)}, bf16[4,14,4,1536]{3,2,1,0:T(4,128)(2,1)}) custom-call(s32[5]{0:T(128)} %in_b.1, s32[5]{0:T(128)} %out_b.1, bf16[4,14,4,1536]{3,2,1,0:T(4,128)(2,1)} %t_ref.1, bf16[768,384]{1,0:T(8,128)(2,1)} %dw_hbm.1, bf16[384,768]{1,0:T(8,128)(2,1)} %uw_hbm.1, bf16[192,192]{1,0:T(8,128)(2,1)} %ow_hbm.1, ...), custom_call_target="tpu_custom_call" | custom-call | tf_op jit(solution)/shard_map/pallas_call | solution.py:365
  24.4 0.0 copy-start
  24.4 2.1 %copy.14 = bf16[4,8,2,3072]{3,2,1,0:T(2,128)(2,1)} copy(bf16[4,8,2,3072]{3,2,1,0:T(2,128)(2,1)} %get-tuple-element.4) | data formatting | bytes 786432
  26.5 0.0 copy-done
  26.5 0.8 %copy.15 = bf16[4,14,4,1536]{3,2,1,0:T(4,128)(2,1)} copy(bf16[4,14,4,1536]{3,2,1,0:T(4,128)(2,1)S(1)} %copy-done) | data formatting | bytes 1376256
Async XLA Ops:
  24.4 2.1 %copy-start = (bf16[4,14,4,1536]{3,2,1,0:T(4,128)(2,1)S(1)}, bf16[4,14,4,1536]{3,2,1,0:T(4,128)(2,1)}, u32[]{:S(2)}) copy-start(bf16[4,14,4,1536]{3,2,1,0:T(4,128)(2,1)} %get-tuple-element.5) | copy-start | bytes 2064388

commit v3 on v2

--- a/solution.py
+++ b/solution.py
@@ -36,17 +36,13 @@
     mo_ref,
     fo_ref,
     comb,
-    west_in,
-    east_in,
+    side_in,
     top_in,
     bot_in,
-    top_w,
-    top_e,
-    bot_w,
-    bot_e,
+    top_c,
+    bot_c,
     tail,
-    tail_w,
-    tail_e,
+    tail_c,
     nrm,
     turn_in,
     turn_merged,
@@ -69,8 +65,9 @@
     mid_lo, mid_hi = HALO, slots // 2
     lat = lax.axis_index("lat")
     lon = lax.axis_index("lon")
-    east = {"lat": lat, "lon": lax.rem(lon + 1, n_lon)}
-    west = {"lat": lat, "lon": lax.rem(lon + n_lon - 1, n_lon)}
+    odd = lax.rem(lon, 2)
+    far = {"lat": lat, "lon": lax.rem(lon + n_lon - 1 + 2 * odd, n_lon)}
+    near = {"lat": lat, "lon": lax.rem(lon + 1 + (n_lon - 2) * odd, n_lon)}
     above = {"lat": jnp.maximum(lat - 1, 0), "lon": lon}
     below = {"lat": jnp.minimum(lat + 1, n_lat - 1), "lon": lon}
     has_above = lat > 0
@@ -78,15 +75,16 @@
 
     loads = [
         pltpu.make_async_copy(dw_hbm, dw, local_sem.at[0]),
-        pltpu.make_async_copy(uw_hbm, uw, local_sem.at[1]),
-        pltpu.make_async_copy(ow_hbm, ow, local_sem.at[2]),
+        pltpu.make_async_copy(uw_hbm.at[:, pl.ds(0, 2 * chan)], uw.at[0], local_sem.at[1]),
+        pltpu.make_async_copy(uw_hbm.at[:, pl.ds(2 * chan, 2 * chan)], uw.at[1], local_sem.at[2]),
+        pltpu.make_async_copy(ow_hbm, ow, local_sem.at[3]),
     ]
     for load in loads:
         load.start()
 
     barrier = pltpu.get_barrier_semaphore()
-    pl.semaphore_signal(barrier, inc=1, device_id=east, device_id_type=MESH)
-    pl.semaphore_signal(barrier, inc=1, device_id=west, device_id_type=MESH)
+    pl.semaphore_signal(barrier, inc=1, device_id=far, device_id_type=MESH)
+    pl.semaphore_signal(barrier, inc=1, device_id=near, device_id_type=MESH)
 
     @pl.when(has_above)
     def _():
@@ -127,24 +125,28 @@
             device_id_type=MESH,
         )
 
+    sides = (odd, 1 - odd)
     spans = [(0, mid_lo), (mid_hi, slots), (mid_lo, mid_hi)]
-    to_east, to_west = [], []
-    for i, (lo, hi) in enumerate(spans):
-        span = pl.ds(lo, hi - lo)
-        held = pl.ds(HALO + lo, hi - lo)
-        to_east.append(remote(comb.at[cols, held], west_in.at[span], i, east))
-        to_west.append(remote(comb.at[1, held], east_in.at[span], 3 + i, west))
-    up = remote(comb.at[pl.ds(1, cols), pl.ds(HALO, HALO)], bot_in, 6, above)
-    down = remote(tail, top_in, 7, below)
-    head = pl.ds(0, HALO)
-    up_w = remote(west_in.at[head], bot_w, 8, above)
-    up_e = remote(east_in.at[head], bot_e, 9, above)
-    down_w = remote(tail_w, top_w, 10, below)
-    down_e = remote(tail_e, top_e, 11, below)
-
-    for i in range(3):
-        to_east[i].start()
-        to_west[i].start()
+    far_copy = remote(
+        comb.at[1 + odd * (cols - 1), pl.ds(HALO, slots)], side_in.at[1 - odd], 0, far
+    )
+    near_copies = [
+        remote(
+            comb.at[cols - odd * (cols - 1), pl.ds(HALO + lo, hi - lo)],
+            side_in.at[odd, pl.ds(lo, hi - lo)],
+            1 + i,
+            near,
+        )
+        for i, (lo, hi) in enumerate(spans)
+    ]
+    up = remote(comb.at[pl.ds(1, cols), pl.ds(HALO, HALO)], bot_in, 4, above)
+    down = remote(tail, top_in, 5, below)
+    up_c = [remote(side_in.at[sides[o], pl.ds(0, HALO)], bot_c.at[o], 6 + o, above) for o in range(2)]
+    down_c = [remote(tail_c.at[o], top_c.at[o], 8 + o, below) for o in range(2)]
+
+    far_copy.start()
+    for copy in near_copies:
+        copy.start()
 
     for x in range(1, cols - 1):
         take_column(x)
@@ -182,7 +184,7 @@
     ug = ug_ref[...][None]
     ub = ub_ref[...][None]
 
-    def compute(j, ms):
+    def compute(base, ms, targets, merged_at):
         nm = len(ms)
         size = LANES_OF_LEVELS * nm * sub
         for k in range(0, nm, 2):
@@ -191,7 +193,7 @@
                 for a in range(2):
                     blocks.append(
                         jnp.concatenate(
-                            [comb[2 * j + c, spots[2 * m + a]].astype(jnp.float32) for m in ms[k : k + 2]],
+                            [comb[base + c, spots[2 * m + a]].astype(jnp.float32) for m in ms[k : k + 2]],
                             axis=0,
                         )
                     )
@@ -202,7 +204,8 @@
                 nrm[at : at + 2 * sub, :] = norm(pieces, dg, db).astype(jnp.bfloat16)
         wide = jnp.dot(nrm[0:size, :], dw[...], preferred_element_type=jnp.float32)
         coarse = wide.astype(jnp.bfloat16)
-        if j < 2:
+        if merged_at is not None:
+            merged_half, j = merged_at
             for i, m in enumerate(ms):
                 if m < 2:
                     continue
@@ -210,11 +213,11 @@
                     at = (level * nm + i) * sub
                     for t in range(2 * chan // TILE):
                         turn_merged[
-                            m - 2, level * 2 * chan // TILE + t, pl.ds(j, sub, stride=cols // 2), :
+                            merged_half * merged_slots + m - 2, level * 2 * chan // TILE + t, pl.ds(j, sub, stride=cols // 2), :
                         ] = wide[at : at + sub, t * TILE : (t + 1) * TILE]
-        for c, x in (((1, 0),), ((0, 1), (1, 2)), ((0, 3),))[j]:
+        for c, x in targets:
             spread = jnp.dot(
-                coarse, uw[:, c * 2 * chan : (c + 1) * 2 * chan], preferred_element_type=jnp.float32
+                coarse, uw[c], preferred_element_type=jnp.float32
             ).astype(jnp.bfloat16)
             spread = spread.astype(jnp.float32)
             for a in range(2):
@@ -257,47 +260,54 @@
         comb[:, 0:HALO] = jnp.zeros((cols + 2, HALO, sub, lanes), jnp.bfloat16)
 
     merged_rows = rows // 2
-    compute(1, list(range(merged_rows)))
-
+    compute(2, list(range(merged_rows)), ((0, 1), (1, 2)), (0, 1))
+
+    def compute_side(o, ms):
+        side = sides[o]
+        compute(side * cols, ms, ((1 - side, side * (cols - 1)),), (side, 0))
+
+    def arrive(o, lo, hi):
+        comb[sides[o] * (cols + 1), HALO + lo : HALO + hi] = side_in[sides[o], lo:hi]
+
+    def pass_corners(o):
+        for i in range(HALO):
+            tail_c[o, i] = comb[sides[o] * (cols + 1), count + i]
+
+        @pl.when(has_above)
+        def _():
+            up_c[o].start()
+
+        @pl.when(has_below)
+        def _():
+            down_c[o].start()
+
+    def take_corners(o):
+        @pl.when(has_above)
+        def _():
+            down_c[o].wait_recv()
+            comb[sides[o] * (cols + 1), 0:HALO] = top_c[o]
+
+        @pl.when(has_below)
+        def _():
+            up_c[o].wait_recv()
+            comb[sides[o] * (cols + 1), HALO + slots : total] = bot_c[o]
+
+    inner = [2, 3]
+    outer = [m for m in range(merged_rows) if m not in inner]
+    far_copy.wait_recv()
+    arrive(0, 0, slots)
+    pass_corners(0)
+    compute_side(0, inner)
+    take_corners(0)
     for i in range(2):
-        lo, hi = spans[i]
-        to_east[i].wait_recv()
-        comb[0, HALO + lo : HALO + hi] = west_in[lo:hi]
-        to_west[i].wait_recv()
-        comb[cols + 1, HALO + lo : HALO + hi] = east_in[lo:hi]
-    for i in range(HALO):
-        tail_w[i] = comb[0, count + i]
-        tail_e[i] = comb[cols + 1, count + i]
-
-    @pl.when(has_above)
-    def _():
-        up_w.start()
-        up_e.start()
-
-    @pl.when(has_below)
-    def _():
-        down_w.start()
-        down_e.start()
-
-    lo, hi = spans[2]
-    to_east[2].wait_recv()
-    comb[0, HALO + lo : HALO + hi] = west_in[lo:hi]
-    to_west[2].wait_recv()
-    comb[cols + 1, HALO + lo : HALO + hi] = east_in[lo:hi]
-
-    @pl.when(has_above)
-    def _():
-        down_w.wait_recv()
-        comb[0, 0:HALO] = top_w[...]
-        down_e.wait_recv()
-        comb[cols + 1, 0:HALO] = top_e[...]
-
-    @pl.when(has_below)
-    def _():
-        up_w.wait_recv()
-        comb[0, HALO + slots : total] = bot_w[...]
-        up_e.wait_recv()
-        comb[cols + 1, HALO + slots : total] = bot_e[...]
+        near_copies[i].wait_recv()
+        arrive(1, *spans[i])
+    pass_corners(1)
+    compute_side(0, outer)
+    near_copies[2].wait_recv()
+    arrive(1, *spans[2])
+    take_corners(1)
+    compute_side(1, list(range(merged_rows)))
 
     def put_out(value, live, slot, out_ref, width, span):
         value = jnp.where(live, value, 0.0).astype(jnp.bfloat16)
@@ -308,28 +318,27 @@
                     [value[t, at : at + width] for t in range(span // TILE)], axis=1
                 )
 
-    compute(0, list(range(merged_rows)))
     count_out = out_b[lat + 1] - out_b[lat]
     for m in range(merged_slots):
         put_out(turn_merged[m], m < count_out, m, mo_ref, cols // 2, 2 * lanes)
-    compute(2, list(range(merged_rows)))
     for k in range(slots):
         put_out(turn_fine[4 - shift + k], k < count, k, fo_ref, cols, lanes)
 
-    for copy in to_east + to_west:
+    far_copy.wait_send()
+    for copy in near_copies:
         copy.wait_send()
 
     @pl.when(has_above)
     def _():
         up.wait_send()
-        up_w.wait_send()
-        up_e.wait_send()
+        for copy in up_c:
+            copy.wait_send()
 
     @pl.when(has_below)
     def _():
         down.wait_send()
-        down_w.wait_send()
-        down_e.wait_send()
+        for copy in down_c:
+            copy.wait_send()
 
 
 def body(
@@ -359,9 +368,8 @@
     smem = pl.BlockSpec(memory_space=pltpu.SMEM)
     vmem = pl.BlockSpec(memory_space=pltpu.VMEM)
     hbm = pl.BlockSpec(memory_space=pl.ANY)
-    column = pltpu.VMEM((slots, sub, lanes), bf16)
     patch = pltpu.VMEM((cols, HALO, sub, lanes), bf16)
-    corner = pltpu.VMEM((HALO, sub, lanes), bf16)
+    corners = pltpu.VMEM((2, HALO, sub, lanes), bf16)
     return pl.pallas_call(
         functools.partial(kernel, n_lat, n_lon),
         out_shape=(
@@ -372,27 +380,23 @@
         out_specs=(vmem, vmem),
         scratch_shapes=[
             pltpu.VMEM((cols + 2, total, sub, lanes), bf16),
-            column,
-            column,
+            pltpu.VMEM((2, slots, sub, lanes), bf16),
             patch,
             patch,
-            corner,
-            corner,
-            corner,
-            corner,
+            corners,
+            corners,
             patch,
-            corner,
-            corner,
+            corners,
             pltpu.VMEM((LANES_OF_LEVELS * rows // 2 * sub, 4 * chan), bf16),
             pltpu.VMEM((slots, lanes // TILE, sub * cols, TILE), jnp.float32),
-            pltpu.VMEM((merged_slots, 2 * lanes // TILE, sub * half_cols, TILE), jnp.float32),
+            pltpu.VMEM((2 * merged_slots, 2 * lanes // TILE, sub * half_cols, TILE), jnp.float32),
             pltpu.VMEM((rows, lanes // TILE, sub * cols, TILE), jnp.float32),
             pltpu.VMEM(down_weight.shape, bf16),
-            pltpu.VMEM(up_weight.shape, bf16),
+            pltpu.VMEM((2, 2 * chan, 2 * chan), bf16),
             pltpu.VMEM(out_weight.shape, bf16),
-            pltpu.SemaphoreType.DMA((3,)),
-            pltpu.SemaphoreType.DMA((12,)),
-            pltpu.SemaphoreType.DMA((12,)),
+            pltpu.SemaphoreType.DMA((4,)),
+            pltpu.SemaphoreType.DMA((10,)),
+            pltpu.SemaphoreType.DMA((10,)),
         ],
         compiler_params=pltpu.CompilerParams(collective_id=0, has_side_effects=True),
     )(

time: 27.5 us -> 28.9 us (1.051)
  Pallas kernels: 23.8 us -> 25.2 us
    pallas_call x1, Pallas kernels: 23.8 us -> 25.2 us  [body(): pl.pallas_call(functools.partial(kernel, n_lat, n_lon), out_shape=(jax.Sh...]
where the time goes in v3:
time: 28.9 us; the launch traced here: 28.7 us
  Pallas kernels  25.2 us (87%)
  local copies, waits for them, and re-layouts  2.93 us (10%)
  between operations  0.65 us (2%)
    pallas_call x1, Pallas kernels, body(): pl.pallas_call(functools.partial(kernel, n_lat, n_lon), out_shape=(jax.Sh...  25.2 us
    unnamed x4, local copies, waits for them, and re-layouts  2.93 us

profile of v3, /device:TPU:1, one launch (start us, length us, event | category | flops | bytes accessed | tf_op | source)
XLA Modules:
  0.0 28.7 jit_solution(7826441419809587745)
XLA Ops:
  0.6 25.2 %shard_map.113 = (bf16[4,8,2,3072]{3,2,1,0:T(2,128)(2,1)}, bf16[4,14,4,1536]{3,2,1,0:T(4,128)(2,1)}) custom-call(s32[5]{0:T(128)} %in_b.1, s32[5]{0:T(128)} %out_b.1, bf16[4,14,4,1536]{3,2,1,0:T(4,128)(2,1)} %t_ref.1, bf16[768,384]{1,0:T(8,128)(2,1)} %dw_hbm.1, bf16[384,768]{1,0:T(8,128)(2,1)} %uw_hbm.1, bf16[192,192]{1,0:T(8,128)(2,1)} %ow_hbm.1, ...), custom_call_target="tpu_custom_call" | custom-call | tf_op jit(solution)/shard_map/pallas_call | solution.py:373
  25.8 0.0 copy-start
  25.8 2.1 %copy.14 = bf16[4,8,2,3072]{3,2,1,0:T(2,128)(2,1)} copy(bf16[4,8,2,3072]{3,2,1,0:T(2,128)(2,1)} %get-tuple-element.4) | data formatting | bytes 786432
  27.9 0.0 copy-done
  27.9 0.8 %copy.15 = bf16[4,14,4,1536]{3,2,1,0:T(4,128)(2,1)} copy(bf16[4,14,4,1536]{3,2,1,0:T(4,128)(2,1)S(1)} %copy-done) | data formatting | bytes 1376256
Async XLA Ops:
  25.8 2.1 %copy-start = (bf16[4,14,4,1536]{3,2,1,0:T(4,128)(2,1)S(1)}, bf16[4,14,4,1536]{3,2,1,0:T(4,128)(2,1)}, u32[]{:S(2)}) copy-start(bf16[4,14,4,1536]{3,2,1,0:T(4,128)(2,1)} %get-tuple-element.5) | copy-start | bytes 2064388

commit v4 on v2

--- a/solution.py
+++ b/solution.py
@@ -394,7 +394,9 @@
             pltpu.SemaphoreType.DMA((12,)),
             pltpu.SemaphoreType.DMA((12,)),
         ],
-        compiler_params=pltpu.CompilerParams(collective_id=0, has_side_effects=True),
+        compiler_params=pltpu.CompilerParams(
+            collective_id=0, has_side_effects=True, vmem_limit_bytes=24 * 1024 * 1024
+        ),
     )(
         in_bounds,
         out_bounds,

time: 27.5 us -> 33.3 us (1.21)
  local copies, waits for them, and re-layouts: 2.93 us -> 9.75 us
  Pallas kernels: 23.8 us -> 22.5 us
    unnamed x4 -> x22, local copies, waits for them, and re-layouts: 2.93 us -> 9.75 us
    pallas_call x1, Pallas kernels: 23.8 us -> 22.5 us  [body(): pl.pallas_call(functools.partial(kernel, n_lat, n_lon), out_shape=(jax.Sh...]
where the time goes in v4:
time: 33.3 us; the launch traced here: 32.9 us
  Pallas kernels  22.5 us (68%)
  local copies, waits for them, and re-layouts  9.75 us (29%)
  between operations  0.66 us (2%)
    pallas_call x1, Pallas kernels, body(): pl.pallas_call(functools.partial(kernel, n_lat, n_lon), out_shape=(jax.Sh...  22.5 us
    unnamed x22, local copies, waits for them, and re-layouts  9.75 us

profile of v4, /device:TPU:1, one launch (start us, length us, event | category | flops | bytes accessed | tf_op | source)
XLA Modules:
  0.0 32.9 jit_solution(16595570478282133816)
XLA Ops:
  0.6 0.0 copy-start
  0.6 1.1 %copy-done = bf16[4,14,4,1536]{3,2,1,0:T(4,128)(2,1)S(1)} copy-done((bf16[4,14,4,1536]{3,2,1,0:T(4,128)(2,1)S(1)}, bf16[4,14,4,1536]{3,2,1,0:T(4,128)(2,1)}, u32[]{:S(2)}) %copy-start) | copy-done | bytes 688152
  1.7 0.0 copy-start.1
  1.7 1.1 %copy-done.1 = bf16[768,384]{1,0:T(8,128)(2,1)S(1)} copy-done((bf16[768,384]{1,0:T(8,128)(2,1)S(1)}, bf16[768,384]{1,0:T(8,128)(2,1)}, u32[]{:S(2)}) %copy-start.1) | copy-done | bytes 589848
  2.8 0.0 copy-start.2
  2.8 1.1 %copy-done.2 = bf16[384,768]{1,0:T(8,128)(2,1)S(1)} copy-done((bf16[384,768]{1,0:T(8,128)(2,1)S(1)}, bf16[384,768]{1,0:T(8,128)(2,1)}, u32[]{:S(2)}) %copy-start.2) | copy-done | bytes 589848
  3.9 0.0 copy-start.3
  3.9 0.9 %copy-done.3 = bf16[192,192]{1,0:T(8,128)(2,1)S(1)} copy-done((bf16[192,192]{1,0:T(8,128)(2,1)S(1)}, bf16[192,192]{1,0:T(8,128)(2,1)}, u32[]{:S(2)}) %copy-start.3) | copy-done | bytes 73752
  4.8 0.0 copy-start.4
  4.8 0.7 %copy-done.4 = f32[768]{0:T(1024)S(1)} copy-done((f32[768]{0:T(1024)S(1)}, f32[768]{0:T(1024)}, u32[]{:S(2)}) %copy-start.4) | copy-done | bytes 3096
  5.4 0.0 copy-start.5
  5.4 0.7 %copy-done.5 = f32[768]{0:T(1024)S(1)} copy-done((f32[768]{0:T(1024)S(1)}, f32[768]{0:T(1024)}, u32[]{:S(2)}) %copy-start.5) | copy-done | bytes 3096
  6.1 0.0 copy-start.6
  6.1 0.7 %copy-done.6 = f32[192]{0:T(256)S(1)} copy-done((f32[192]{0:T(256)S(1)}, f32[192]{0:T(256)}, u32[]{:S(2)}) %copy-start.6) | copy-done | bytes 792
  6.8 0.0 copy-start.7
  6.8 0.7 %copy-done.7 = f32[192]{0:T(256)S(1)} copy-done((f32[192]{0:T(256)S(1)}, f32[192]{0:T(256)}, u32[]{:S(2)}) %copy-start.7) | copy-done | bytes 792
  7.5 0.0 copy-start.8
  7.5 0.7 %copy-done.8 = s32[5]{0:T(128)S(1)} copy-done((s32[5]{0:T(128)S(1)}, s32[5]{0:T(128)}, u32[]{:S(2)}) %copy-start.8) | copy-done | bytes 44
  8.1 0.0 copy-start.9
  8.1 0.7 %copy-done.9 = s32[5]{0:T(128)S(1)} copy-done((s32[5]{0:T(128)S(1)}, s32[5]{0:T(128)}, u32[]{:S(2)}) %copy-start.9) | copy-done | bytes 44
  8.8 22.5 %shard_map.113 = (bf16[4,8,2,3072]{3,2,1,0:T(2,128)(2,1)S(1)}, bf16[4,14,4,1536]{3,2,1,0:T(4,128)(2,1)S(1)}) custom-call(s32[5]{0:T(128)S(1)} %copy-done.8, s32[5]{0:T(128)S(1)} %copy-done.9, bf16[4,14,4,1536]{3,2,1,0:T(4,128)(2,1)S(1)} %copy-done, bf16[768,384]{1,0:T(8,128)(2,1)S(1)} %copy-done.1, bf16[384,768]{1,0:T(8,128)(2,1)S(1)} %copy-done.2, ...), custom_call_target="tpu_custom_call" | custom-call | tf_op jit(solution)/shard_map/pallas_call | solution.py:365
  31.3 0.7 %copy.14 = bf16[4,8,2,3072]{3,2,1,0:T(2,128)(2,1)} copy(bf16[4,8,2,3072]{3,2,1,0:T(2,128)(2,1)S(1)} %get-tuple-element.4) | data formatting | bytes 786432
  32.1 0.8 %copy.15 = bf16[4,14,4,1536]{3,2,1,0:T(4,128)(2,1)} copy(bf16[4,14,4,1536]{3,2,1,0:T(4,128)(2,1)S(1)} %get-tuple-element.5) | data formatting | bytes 1376256
Async XLA Ops:
  0.6 1.1 %copy-start = (bf16[4,14,4,1536]{3,2,1,0:T(4,128)(2,1)S(1)}, bf16[4,14,4,1536]{3,2,1,0:T(4,128)(2,1)}, u32[]{:S(2)}) copy-start(bf16[4,14,4,1536]{3,2,1,0:T(4,128)(2,1)} %t_ref.1) | copy-start | bytes 2064388
  1.7 1.1 %copy-start.1 = (bf16[768,384]{1,0:T(8,128)(2,1)S(1)}, bf16[768,384]{1,0:T(8,128)(2,1)}, u32[]{:S(2)}) copy-start(bf16[768,384]{1,0:T(8,128)(2,1)} %dw_hbm.1) | copy-start | bytes 1769476
  2.8 1.1 %copy-start.2 = (bf16[384,768]{1,0:T(8,128)(2,1)S(1)}, bf16[384,768]{1,0:T(8,128)(2,1)}, u32[]{:S(2)}) copy-start(bf16[384,768]{1,0:T(8,128)(2,1)} %uw_hbm.1) | copy-start | bytes 1769476
  3.9 0.9 %copy-start.3 = (bf16[192,192]{1,0:T(8,128)(2,1)S(1)}, bf16[192,192]{1,0:T(8,128)(2,1)}, u32[]{:S(2)}) copy-start(bf16[192,192]{1,0:T(8,128)(2,1)} %ow_hbm.1) | copy-start | bytes 221188
  4.8 0.7 %copy-start.4 = (f32[768]{0:T(1024)S(1)}, f32[768]{0:T(1024)}, u32[]{:S(2)}) copy-start(f32[768]{0:T(1024)} %dg_ref.1) | copy-start | bytes 9220
  5.4 0.7 %copy-start.5 = (f32[768]{0:T(1024)S(1)}, f32[768]{0:T(1024)}, u32[]{:S(2)}) copy-start(f32[768]{0:T(1024)} %db_ref.1) | copy-start | bytes 9220
  6.1 0.7 %copy-start.6 = (f32[192]{0:T(256)S(1)}, f32[192]{0:T(256)}, u32[]{:S(2)}) copy-start(f32[192]{0:T(256)} %ug_ref.1) | copy-start | bytes 2308
  6.8 0.7 %copy-start.7 = (f32[192]{0:T(256)S(1)}, f32[192]{0:T(256)}, u32[]{:S(2)}) copy-start(f32[192]{0:T(256)} %ub_ref.1) | copy-start | bytes 2308
  7.5 0.7 %copy-start.8 = (s32[5]{0:T(128)S(1)}, s32[5]{0:T(128)}, u32[]{:S(2)}) copy-start(s32[5]{0:T(128)} %in_b.1) | copy-start | bytes 64
  8.1 0.7 %copy-start.9 = (s32[5]{0:T(128)S(1)}, s32[5]{0:T(128)}, u32[]{:S(2)}) copy-start(s32[5]{0:T(128)} %out_b.1) | copy-start | bytes 64
